TPU v7x, 32 devices: a whole 2x2x4 slice. The times are simulated.
32 devices in a mesh: region: 8 (over z, core), feat: 4 (over y, x).
Axes of the slice: x: 2, y: 2, z: 4, core: 2. Of those that a mesh axis runs over, the one named last changes fastest.
Arguments:
- node_lat: bfloat16 [3072, 512], P(('region', 'feat')), may hold values from -6 to 6
- edge_lat: bfloat16 [24576, 512], P(('region', 'feat')), may hold values from -6 to 6
- receiver_row: int32 [24576], P('region'), may hold values from 0 to 383
- sender_slot: int32 [24576], P('region'), may hold values from 0 to 511, as said below
- send_rows: int32 [8, 8, 16], P('region'), may hold values from 0 to 383
- w_edge_in: bfloat16 [3, 512, 512], P(None, 'feat'), may hold values from -0.15625 to 0.15625
- w_edge_out: bfloat16 [512, 512], P('feat'), may hold values from -0.25 to 0.25
- w_node_in: bfloat16 [2, 512, 512], P(None, 'feat'), may hold values from -0.1875 to 0.1875
- w_node_out: bfloat16 [512, 512], P('feat'), may hold values from -0.25 to 0.25
- edge_gain: float32 [512], P('feat'), may hold values from 0.1 to 1.9
- node_gain: float32 [512], P('feat'), may hold values from 0.1 to 1.9
- node_cot: bfloat16 [3072, 512], P(('region', 'feat')), may hold values from -6 to 6
- edge_cot: bfloat16 [24576, 512], P(('region', 'feat')), may hold values from -6 to 6
Outputs:
- node_new: bfloat16 [3072, 512], P(('region', 'feat'))
- edge_new: bfloat16 [24576, 512], P(('region', 'feat'))
- node_grad: float32 [3072, 512], P(('region', 'feat'))
- edge_grad: float32 [24576, 512], P(('region', 'feat'))
- grad_edge_in: float32 [3, 512, 512], P(None, 'feat')
- grad_edge_out: float32 [512, 512], P('feat')
- grad_node_in: float32 [2, 512, 512], P(None, 'feat')
- grad_node_out: float32 [512, 512], P('feat')
Inputs may be any that keep to these rules, and one draw needn't show every extreme that they name: `receiver_row`: edge e lies in region e // 3072; its receiver is that row of the region's 384 nodes. `sender_slot`: A value below 384 is a row of the edge's own region; a value 384 + p * 16 + s names the node that region p lists in slot s for the edge's region, and p is never the edge's own region. send_rows[p, r, s] is a row of region p's 384 nodes.
All inputs are finite; a program needn't handle non-finite values.
Results may differ from a plain program's by a relative error of at most 0.02.
Values may be sent and summed in bfloat16 or wider, within the bound.
No kernel may reach another device: no remote copies, remote signals or barrier semaphores. Data moves between devices by JAX's collectives and lax.ppermute only.
A program may use at most 64 MiB of HBM per device.

v0:
```python
import jax
import jax.numpy as jnp
from jax import lax
from jax.sharding import PartitionSpec as P

EPSILON = 1e-05


def apply_swish(values):
    return values * jax.nn.sigmoid(values)


def swish_slope(values):
    sigmoid_value = jax.nn.sigmoid(values)
    return sigmoid_value * (1.0 + values * (1.0 - sigmoid_value))


def layer_norm(values, gain_values, breadth):
    sums = jnp.sum(values, axis=1)
    squares = jnp.sum(values * values, axis=1)
    average = sums[:, None] / breadth
    variance = squares[:, None] / breadth - average * average
    inverse = lax.rsqrt(variance + EPSILON)
    normed = (values - average) * inverse
    return (normed, inverse, normed * gain_values)


def layer_norm_back(cotangent, normed, inverse, gain_values, breadth):
    scaled = cotangent * gain_values
    first_sum = jnp.sum(scaled, axis=1)
    second_sum = jnp.sum(scaled * normed, axis=1)
    return (
        inverse * (scaled - first_sum[:, None] / breadth - normed * (second_sum[:, None] / breadth))
    ).astype(jnp.bfloat16)


def matmul_back(first_operand, second_operand):
    return lax.dot_general(
        first_operand, second_operand, (((1,), (1,)), ((), ())), preferred_element_type=jnp.float32
    )


def transposed(first_operand, second_operand):
    return lax.dot_general(
        first_operand, second_operand, (((0,), (0,)), ((), ())), preferred_element_type=jnp.float32
    )


def split_parts(values):
    upper_part = lax.optimization_barrier(values.astype(jnp.bfloat16))
    lower_part = (values - upper_part.astype(jnp.float32)).astype(jnp.bfloat16)
    return (upper_part, lower_part)


def shards(
    node_lat,
    edge_lat,
    receiver_row,
    sender_slot,
    send_rows,
    w_edge_in,
    w_edge_out,
    w_node_in,
    w_node_out,
    edge_gain,
    node_gain,
    node_cot,
    edge_cot,
):
    node_latent_rows = node_lat
    edge_latent_rows = edge_lat
    node_cot_rows = node_cot
    edge_cot_rows = edge_cot
    node_lat, edge_lat, node_cot, edge_cot = (
        lax.all_to_all(node_latent_rows, "feat", split_axis=1, concat_axis=0, tiled=True),
        lax.all_to_all(edge_latent_rows, "feat", split_axis=1, concat_axis=0, tiled=True),
        lax.all_to_all(node_cot_rows, "feat", split_axis=1, concat_axis=0, tiled=True),
        lax.all_to_all(edge_cot_rows, "feat", split_axis=1, concat_axis=0, tiled=True),
    )
    breadth = w_edge_out.shape[1]
    portion = w_edge_out.shape[0]
    node_count = node_lat.shape[0]
    edge_count = edge_lat.shape[0]
    feat_count = lax.axis_size("feat")
    feat_here = lax.axis_index("feat")
    offset = feat_here * portion
    stacked = jnp.concatenate([w_edge_in, w_edge_out[None], w_node_in, w_node_out[None]], axis=0)
    send_list = send_rows[0]
    outgoing = node_lat[send_list]
    incoming = lax.all_to_all(outgoing, "region", split_axis=0, concat_axis=0, tiled=True)
    lookup_table = jnp.concatenate([node_lat, incoming.reshape(-1, portion)], axis=0)
    senders = lookup_table[sender_slot]
    receivers = node_lat[receiver_row]
    node_ids = jnp.arange(node_count, dtype=jnp.int32)
    incidence = (node_ids[:, None] == receiver_row[None, :]).astype(jnp.bfloat16)
    edge_share = edge_count // feat_count
    full_weights = lax.all_gather(stacked, "feat", axis=1, tiled=True)
    full_gains = lax.all_gather(
        jnp.stack([edge_gain, node_gain], axis=0), "feat", axis=1, tiled=True
    )
    lookup_full = lax.all_gather(lookup_table, "feat", axis=1, tiled=True)
    local_receivers = lax.dynamic_slice_in_dim(receiver_row, feat_here * edge_share, edge_share)
    local_senders = lax.dynamic_slice_in_dim(sender_slot, feat_here * edge_share, edge_share)
    sender_rows = lookup_full[local_senders]
    receiver_rows = lookup_full[local_receivers]
    pre_hidden_rows = (
        jnp.dot(edge_latent_rows, full_weights[0], preferred_element_type=jnp.float32)
        + jnp.dot(sender_rows, full_weights[1], preferred_element_type=jnp.float32)
        + jnp.dot(receiver_rows, full_weights[2], preferred_element_type=jnp.float32)
    )
    hidden_rows = apply_swish(pre_hidden_rows).astype(jnp.bfloat16)
    edge_mix_rows = jnp.dot(hidden_rows, full_weights[3], preferred_element_type=jnp.float32)
    edge_normed_rows, edge_inverse_rows, edge_update_rows = layer_norm(
        edge_mix_rows, full_gains[0], breadth
    )
    edge_new_rows = (edge_latent_rows.astype(jnp.float32) + edge_update_rows).astype(jnp.bfloat16)
    row_incidence = (node_ids[:, None] == local_receivers[None, :]).astype(jnp.bfloat16)
    pooled_rows = lax.psum_scatter(
        jnp.dot(row_incidence, edge_new_rows, preferred_element_type=jnp.float32).astype(
            jnp.bfloat16
        ),
        "feat",
        scatter_dimension=0,
        tiled=True,
    )
    node_pre_rows = jnp.dot(
        node_latent_rows, full_weights[4], preferred_element_type=jnp.float32
    ) + jnp.dot(pooled_rows, full_weights[5], preferred_element_type=jnp.float32)
    node_hidden_rows = apply_swish(node_pre_rows).astype(jnp.bfloat16)
    node_mix_rows = jnp.dot(node_hidden_rows, full_weights[6], preferred_element_type=jnp.float32)
    node_normed_rows, node_inverse_rows, node_update_rows = layer_norm(
        node_mix_rows, full_gains[1], breadth
    )
    node_new_rows = (node_latent_rows.astype(jnp.float32) + node_update_rows).astype(jnp.bfloat16)
    node_mix_grad_rows = layer_norm_back(
        node_cot_rows.astype(jnp.float32),
        node_normed_rows,
        node_inverse_rows,
        full_gains[1],
        breadth,
    )
    node_pre_grad_rows = (
        matmul_back(node_mix_grad_rows, full_weights[6]) * swish_slope(node_pre_rows)
    ).astype(jnp.bfloat16)
    node_pre_wide, node_mix_wide = (
        lax.all_gather(node_pre_grad_rows, "feat", axis=0, tiled=True),
        lax.all_gather(node_mix_grad_rows, "feat", axis=0, tiled=True),
    )
    pooled_full = matmul_back(node_pre_wide, full_weights[5])
    edge_total_rows = edge_cot_rows.astype(jnp.float32) + pooled_full[local_receivers]
    edge_mix_grad_rows = layer_norm_back(
        edge_total_rows, edge_normed_rows, edge_inverse_rows, full_gains[0], breadth
    )
    pre_grad_rows = (
        matmul_back(edge_mix_grad_rows, full_weights[3]) * swish_slope(pre_hidden_rows)
    ).astype(jnp.bfloat16)
    pre_wide, edge_mix_wide = (
        lax.all_gather(pre_grad_rows, "feat", axis=0, tiled=True),
        lax.all_gather(edge_mix_grad_rows, "feat", axis=0, tiled=True),
    )
    pooled_grad = lax.dynamic_slice_in_dim(pooled_full, offset, portion, 1)
    edge_total = edge_cot.astype(jnp.float32) + pooled_grad[receiver_row]
    node_hidden, pooled, hidden = (
        lax.all_to_all(node_hidden_rows, "feat", split_axis=1, concat_axis=0, tiled=True),
        lax.all_to_all(pooled_rows, "feat", split_axis=1, concat_axis=0, tiled=True),
        lax.all_to_all(hidden_rows, "feat", split_axis=1, concat_axis=0, tiled=True),
    )
    grad_node_second_layer = transposed(node_hidden, node_mix_wide)
    node_direct = matmul_back(node_pre_wide, w_node_in[0])
    grad_node_latent = transposed(node_lat, node_pre_wide)
    grad_node_pooled = transposed(pooled, node_pre_wide)
    grad_edge_second_layer = transposed(hidden, edge_mix_wide)
    edge_grad = edge_total + matmul_back(pre_wide, w_edge_in[0])
    sender_grad = matmul_back(pre_wide, w_edge_in[1])
    grad_edge_latent = transposed(edge_lat, pre_wide)
    grad_edge_sender = transposed(senders, pre_wide)
    upper_part, lower_part = split_parts(matmul_back(pre_wide, w_edge_in[2]))
    receiver_grad = jnp.dot(incidence, upper_part, preferred_element_type=jnp.float32) + jnp.dot(
        incidence, lower_part, preferred_element_type=jnp.float32
    )
    grad_edge_receiver = transposed(receivers, pre_wide)
    table_grad = jax.ops.segment_sum(sender_grad, sender_slot, num_segments=lookup_table.shape[0])
    remote_grad = table_grad[node_count:].reshape(send_list.shape[0], send_list.shape[1], portion)
    returned = lax.all_to_all(
        remote_grad.astype(jnp.bfloat16), "region", split_axis=0, concat_axis=0, tiled=True
    ).astype(remote_grad.dtype)
    node_grad = (
        node_cot.astype(jnp.float32)
        + node_direct
        + receiver_grad
        + table_grad[:node_count]
        + jax.ops.segment_sum(
            returned.reshape(-1, portion), send_list.reshape(-1), num_segments=node_count
        )
    )
    node_grad_out, edge_grad_out = (
        lax.all_to_all(
            node_grad.astype(jnp.bfloat16), "feat", split_axis=0, concat_axis=1, tiled=True
        ).astype(node_grad.dtype),
        lax.all_to_all(
            edge_grad.astype(jnp.bfloat16), "feat", split_axis=0, concat_axis=1, tiled=True
        ).astype(edge_grad.dtype),
    )
    summed_grads = (
        lax.psum(
            jnp.stack([grad_edge_latent, grad_edge_sender, grad_edge_receiver], axis=0).astype(
                jnp.bfloat16
            ),
            "region",
        ).astype(jnp.float32),
        lax.psum(grad_edge_second_layer.astype(jnp.bfloat16), "region").astype(jnp.float32),
        lax.psum(
            jnp.stack([grad_node_latent, grad_node_pooled], axis=0).astype(jnp.bfloat16), "region"
        ).astype(jnp.float32),
        lax.psum(grad_node_second_layer.astype(jnp.bfloat16), "region").astype(jnp.float32),
    )
    edge_norm = 1.0 / jnp.sqrt(jnp.float32(edge_count * lax.axis_size("region")))
    node_norm = 1.0 / jnp.sqrt(jnp.float32(node_count * lax.axis_size("region")))
    return (
        node_new_rows,
        edge_new_rows,
        node_grad_out,
        edge_grad_out,
        summed_grads[0] * edge_norm,
        summed_grads[1] * edge_norm,
        summed_grads[2] * node_norm,
        summed_grads[3] * node_norm,
    )


def solution(mesh):
    in_specs = (
        P(("region", "feat"), None),
        P(("region", "feat"), None),
        P("region"),
        P("region"),
        P("region", None, None),
        P(None, "feat", None),
        P("feat", None),
        P(None, "feat", None),
        P("feat", None),
        P("feat"),
        P("feat"),
        P(("region", "feat"), None),
        P(("region", "feat"), None),
    )
    out_specs = (
        P(("region", "feat"), None),
        P(("region", "feat"), None),
        P(("region", "feat"), None),
        P(("region", "feat"), None),
        P(None, "feat", None),
        P("feat", None),
        P(None, "feat", None),
        P("feat", None),
    )
    return jax.shard_map(shards, mesh=mesh, in_specs=in_specs, out_specs=out_specs, check_vma=False)
```

profile of v0, /device:TPU:0, one launch (start us, length us, event | category | flops | bytes accessed | tf_op | source)
XLA Modules:
  0.0 344.5 jit_solution(10065554357982523741)
XLA Ops:
  7.2 2.3 pad_maximum_fusion
  10.3 5.2 %all-to-all-start = ((bf16[96,4,128]{2,0,1:T(8,128)(2,1)}), bf16[96,4,128]{2,0,1:T(8,128)(2,1)S(1)}, u32[]{:S(2)}, u32[]{:S(2)}) async-start(bf16[96,4,128]{2,0,1:T(8,128)(2,1)} %copy_bitcast_fusion.6), calls=%async_computation | async-start | bytes 196608 | tf_op jit(solution)/shard_map/all_to_all | solution.py:75
  16.7 8.7 %all_gather.23 = f32[2,512]{1,0:T(2,128)S(1)} all-gather(f32[2,128]{1,0:T(2,128)S(1)} %pad_maximum_fusion.4), channel_id=1, replica_groups=mesh['region'=8,'feat'=4] {'feat'}, dimensions={1}, use_global_device_ids=true | all-gather | bytes 5120 | tf_op jit(solution)/shard_map/all_gather | solution.py:98
  27.0 4.9 %all-to-all-start.1 = ((bf16[8,16,128]{2,1,0:T(8,128)(2,1)}), bf16[8,16,128]{2,1,0:T(8,128)(2,1)S(1)}, u32[]{:S(2)}, u32[]{:S(2)}) async-start(bf16[8,16,128]{2,1,0:T(8,128)(2,1)} %bitcast.10), calls=%async_computation.1 | async-start | bytes 65536 | tf_op jit(solution)/shard_map/all_to_all | solution.py:90
  32.0 5.7 %all-to-all-done.1 = bf16[8,16,128]{2,1,0:T(8,128)(2,1)S(1)} async-done(((bf16[8,16,128]{2,1,0:T(8,128)(2,1)}), bf16[8,16,128]{2,1,0:T(8,128)(2,1)S(1)}, u32[]{:S(2)}, u32[]{:S(2)}) %all-to-all-start.1) | async-done | bytes 32800 | tf_op jit(solution)/shard_map/all_to_all | solution.py:90
  37.7 15.3 %all_gather.22 = bf16[512,512]{1,0:T(8,128)(2,1)S(1)} all-gather(bf16[512,128]{1,0:T(8,128)(2,1)S(1)} %pad_maximum_fusion.3), channel_id=1, replica_groups=mesh['region'=8,'feat'=4] {'feat'}, dimensions={1}, use_global_device_ids=true | all-gather | bytes 655360 | tf_op jit(solution)/shard_map/all_gather | solution.py:101
  53.0 2.7 gather_fusion.2
  55.7 2.7 gather_fusion.1
  58.3 7.1 %all-gather.4.cloned.1.call-done = bf16[7,512,512]{2,1,0:T(8,128)(2,1)} async-done(((bf16[7,128,512]{2,1,0:T(8,128)(2,1)}), bf16[7,512,512]{2,1,0:T(8,128)(2,1)}) %all-gather.4.cloned.1.call-update) | async-done | bytes 3670032 | tf_op jit(solution)/shard_map/all_gather | solution.py:97
  65.5 1.7 fusion.18
  67.1 1.7 fusion.17
  68.8 3.0 multiply_convert_fusion.2
  71.8 2.0 fusion.42
  78.7 22.3 %reduce-scatter.2.cloned.1.call-done = bf16[96,512]{1,0:T(8,128)(2,1)} async-done(((bf16[384,512]{1,0:T(8,128)(2,1)}), bf16[96,512]{1,0:T(8,128)(2,1)}) %reduce-scatter.2.cloned.1.call-update) | async-done | bytes 98320 | tf_op jit(solution)/shard_map/reduce_scatter | solution.py:118
  107.3 9.9 %all_gather.24 = bf16[384,512]{1,0:T(8,128)(2,1)S(1)} all-gather(bf16[96,512]{1,0:T(8,128)(2,1)S(1)} %fusion.10), channel_id=1, replica_groups=mesh['region'=8,'feat'=4] {'feat'}, dimensions={0}, use_global_device_ids=true | all-gather | bytes 491520 | tf_op jit(solution)/shard_map/all_gather | solution.py:146
  117.2 1.6 fusion.20
  118.8 3.2 gather_fusion.3
  122.0 3.1 copy.58
  125.0 2.2 fusion.41
  128.8 3.4 %multiply_convert_fusion = bf16[768,512]{0,1:T(8,128)(2,1)} fusion(f32[768,512]{0,1:T(8,128)} %get-tuple-element.55, bf16[768,512]{0,1:T(8,128)(2,1)} %multiply_convert_fusion.1, bf16[7,512,512]{2,1,0:T(8,128)(2,1)} %all-gather.4.cloned.1.call-done), kind=kOutput, calls=%fused_computation.22 | convolution fusion | flops 406192128 | bytes 3670016 | tf_op jit(solution)/shard_map/dot_general | solution.py:38
  132.3 7.6 %all_to_all.157 = bf16[96,4,128]{2,0,1:T(8,128)(2,1)S(1)} all-to-all(bf16[96,4,128]{2,0,1:T(8,128)(2,1)S(1)} %copy_bitcast_fusion.5), channel_id=1, replica_groups=mesh['region'=8,'feat'=4] {'feat'}, dimensions={1} | all-to-all | bytes 196608 | tf_op jit(solution)/shard_map/all_to_all | solution.py:77
  139.9 3.5 %all-to-all-start.7 = ((bf16[768,4,128]{0,2,1:T(8,128)(2,1)}), bf16[768,4,128]{0,2,1:T(8,128)(2,1)S(1)}, u32[]{:S(2)}, u32[]{:S(2)}) async-start(bf16[768,4,128]{0,2,1:T(8,128)(2,1)} %bitcast.35), calls=%async_computation.8 | async-start | bytes 1572864 | tf_op jit(solution)/shard_map/all_to_all | solution.py:76
  144.7 11.5 %gather_fusion.6 = bf16[3072,128]{1,0:T(8,128)(2,1)} fusion(bf16[384,128]{1,0:T(8,128)(2,1)S(1)} %bitcast.174, s32[3072]{0:T(1024)S(1)} %fusion.38), kind=kCustom, calls=%fused_computation.6 | custom fusion | bytes 1585152 | tf_op jit(solution)/shard_map/gather | solution.py:93
  156.9 11.5 %gather_fusion.5 = bf16[3072,128]{1,0:T(8,128)(2,1)} fusion(bf16[512,128]{1,0:T(8,128)(2,1)S(1)} %pad_maximum_fusion.3, s32[3072]{0:T(1024)S(1)} %fusion.39), kind=kCustom, calls=%fused_computation.5 | custom fusion | bytes 1585152 | tf_op jit(solution)/shard_map/gather | solution.py:92
  168.4 4.5 %all-to-all-start.5 = ((bf16[768,4,128]{2,0,1:T(8,128)(2,1)}), bf16[768,4,128]{2,0,1:T(8,128)(2,1)}, u32[]{:S(2)}, u32[]{:S(2)}) async-start(bf16[768,4,128]{2,0,1:T(8,128)(2,1)} %copy_bitcast_fusion.1), calls=%async_computation.6 | async-start | bytes 1572864 | tf_op jit(solution)/shard_map/all_to_all | solution.py:78
  176.4 10.9 %gather_fusion.4 = f32[3072,128]{1,0:T(8,128)} fusion(f32[384,128]{1,0:T(8,128)S(1)} %constant_dynamic-slice_fusion, s32[3072]{0:T(1024)S(1)} %fusion.38), kind=kCustom, calls=%fused_computation.4 | custom fusion | bytes 3158016 | tf_op jit(solution)/shard_map/gather | solution.py:162
  189.0 2.6 all-to-all-done.5
  191.6 3.3 all-to-all-start.9
  194.9 2.9 bitcast_add_fusion
  197.8 13.4 %all_gather.27 = bf16[384,512]{1,0:T(8,128)(2,1)S(1)} all-gather(bf16[96,512]{1,0:T(8,128)(2,1)S(1)} %get-tuple-element.46), channel_id=1, replica_groups=mesh['region'=8,'feat'=4] {'feat'}, dimensions={0}, use_global_device_ids=true | all-gather | bytes 491520 | tf_op jit(solution)/shard_map/all_gather | solution.py:147
  211.2 3.3 all-to-all-start.10
  215.6 4.7 %all-to-all-done.10 = bf16[96,4,128]{2,0,1:T(8,128)(2,1)S(1)} async-done(((bf16[96,4,128]{2,0,1:T(8,128)(2,1)}), bf16[96,4,128]{2,0,1:T(8,128)(2,1)S(1)}, u32[]{:S(2)}, u32[]{:S(2)}) %all-to-all-start.10) | async-done | bytes 98336 | tf_op jit(solution)/shard_map/all_to_all | solution.py:164
  220.3 4.2 %all-to-all-start.8 = ((bf16[768,4,128]{2,0,1:T(8,128)(2,1)}), bf16[768,4,128]{2,0,1:T(8,128)(2,1)}, u32[]{:S(2)}, u32[]{:S(2)}) async-start(bf16[768,4,128]{2,0,1:T(8,128)(2,1)} %copy.67), calls=%async_computation.9 | async-start | bytes 1572864 | tf_op jit(solution)/shard_map/all_to_all | solution.py:166
  225.5 3.1 fusion.45
  229.7 1.6 fusion.15
  231.3 1.6 fusion.14
  232.9 3.1 fusion.25
  236.0 1.6 fusion.6
  237.6 17.3 %scatter_custom_fusion = f32[512,128]{1,0:T(8,128)S(1)} fusion(s32[3072]{0:T(1024)S(1)} %copy-done.23, f32[3072,128]{1,0:T(8,128)} %fusion.25, f32[]{:T(128)} %constant.20.clone.1), kind=kCustom, calls=%fused_computation.95 | custom fusion | flops 393216 | bytes 262656 | tf_op jit(solution)/shard_map/scatter-add | solution.py:182
  255.5 2.1 fusion.9
  257.6 2.8 fusion.13
  260.4 4.8 %all-to-all-start.3 = ((bf16[8,16,128]{2,1,0:T(8,128)(2,1)}), bf16[8,16,128]{2,1,0:T(8,128)(2,1)S(1)}, u32[]{:S(2)}, u32[]{:S(2)}) async-start(bf16[8,16,128]{2,1,0:T(8,128)(2,1)} %bitcast.26), calls=%async_computation.4 | async-start | bytes 65536 | tf_op jit(solution)/shard_map/all_to_all | solution.py:184
  265.3 4.0 %convolution_convert_fusion.6 = bf16[128,512]{1,0:T(8,128)(2,1)} fusion(bf16[3072,128]{1,0:T(8,128)(2,1)} %bitcast.44, bf16[3072,512]{0,1:T(8,128)(2,1)} %all-gather.8.cloned.1.call-done), kind=kOutput, calls=%fused_computation.45 | convolution fusion | flops 402718720 | bytes 4063232 | tf_op jit(solution)/shard_map/dot_general | solution.py:44
  273.0 4.1 %all-to-all-start.4 = ((bf16[4,96,128]{2,1,0:T(8,128)(2,1)}), bf16[4,96,128]{2,1,0:T(8,128)(2,1)S(1)}, u32[]{:S(2)}, u32[]{:S(2)}) async-start(bf16[4,96,128]{2,1,0:T(8,128)(2,1)} %bitcast.28), calls=%async_computation.5 | async-start | bytes 196608 | tf_op jit(solution)/shard_map/all_to_all | solution.py:197
  277.1 3.4 fusion.2
  280.6 1.5 all-to-all-done.4
  282.1 3.5 %all-to-all-start.6 = ((bf16[4,768,128]{2,1,0:T(8,128)(2,1)}), bf16[4,768,128]{2,1,0:T(8,128)(2,1)S(1)}, u32[]{:S(2)}, u32[]{:S(2)}) async-start(bf16[4,768,128]{2,1,0:T(8,128)(2,1)} %bitcast.176), calls=%async_computation.7 | async-start | bytes 1572864 | tf_op jit(solution)/shard_map/all_to_all | solution.py:200
  286.3 44.6 %all-reduce.3.cloned.1.call-done = (bf16[3,128,512]{1,2,0:T(8,128)(2,1)}, bf16[128,512]{1,0:T(8,128)(2,1)}, bf16[2,128,512]{1,2,0:T(8,128)(2,1)}, bf16[128,512]{1,0:T(8,128)(2,1)}) async-done(((bf16[3,128,512]{1,2,0:T(8,128)(2,1)}, bf16[128,512]{1,0:T(8,128)(2,1)}, bf16[2,128,512]{1,2,0:T(8,128)(2,1)}, bf16[128,512]{1,0:T(8,128)(2,1)}), (bf16[3,128,512]{1,2,0:T(8,128)(2,1)}, bf16[128,512]{1,0:T(8,128)(2,1)}, ...) | async-done | bytes 917520 | tf_op jit(solution)/shard_map/psum | solution.py:205
  (131 shorter events, 38.5 us)
Async XLA Ops:
  7.2 2.4 copy-start.12
  7.2 58.3 %all-gather.4.cloned.1.call-start = ((), (), s32[]{:S(2)}) async-start(), calls=%async_computation.12 | async-start | bytes 4587520 | tf_op jit(solution)/shard_map/all_gather | solution.py:97
  7.2 8.2 %copy-start.6 = (bf16[768,512]{1,0:T(8,128)(2,1)S(1)}, bf16[768,512]{1,0:T(8,128)(2,1)}, u32[]{:S(2)}) copy-start(bf16[768,512]{1,0:T(8,128)(2,1)} %param.14) | copy-start | bytes 2359300
  9.6 7.1 %copy-start.24 = (s32[1,8,16]{2,1,0:T(8,128)S(1)}, s32[1,8,16]{2,1,0:T(8,128)}, u32[]{:S(2)}) copy-start(s32[1,8,16]{2,1,0:T(8,128)} %param.17) | copy-start | bytes 1540
  9.6 7.2 %copy-start.25 = (f32[128]{0:T(128)S(1)}, f32[128]{0:T(128)}, u32[]{:S(2)}) copy-start(f32[128]{0:T(128)} %param.23) | copy-start | bytes 1540
  9.6 7.2 %copy-start.26 = (f32[128]{0:T(128)S(1)}, f32[128]{0:T(128)}, u32[]{:S(2)}) copy-start(f32[128]{0:T(128)} %param.22) | copy-start | bytes 1540
  9.6 15.9 %copy-start.22 = (s32[3072]{0:T(1024)S(1)}, s32[3072]{0:T(1024)}, u32[]{:S(2)}) copy-start(s32[3072]{0:T(1024)} %param.15) | copy-start | bytes 36868
  9.6 16.0 %copy-start.23 = (s32[3072]{0:T(1024)S(1)}, s32[3072]{0:T(1024)}, u32[]{:S(2)}) copy-start(s32[3072]{0:T(1024)} %param.16) | copy-start | bytes 36868
  10.3 15.4 %all-to-all-start = ((bf16[96,4,128]{2,0,1:T(8,128)(2,1)}), bf16[96,4,128]{2,0,1:T(8,128)(2,1)S(1)}, u32[]{:S(2)}, u32[]{:S(2)}) async-start(bf16[96,4,128]{2,0,1:T(8,128)(2,1)} %copy_bitcast_fusion.6), calls=%async_computation | async-start | bytes 196608 | tf_op jit(solution)/shard_map/all_to_all | solution.py:75
  27.0 10.7 %all-to-all-start.1 = ((bf16[8,16,128]{2,1,0:T(8,128)(2,1)}), bf16[8,16,128]{2,1,0:T(8,128)(2,1)S(1)}, u32[]{:S(2)}, u32[]{:S(2)}) async-start(bf16[8,16,128]{2,1,0:T(8,128)(2,1)} %bitcast.10), calls=%async_computation.1 | async-start | bytes 65536 | tf_op jit(solution)/shard_map/all_to_all | solution.py:90
  31.9 69.1 %reduce-scatter.2.cloned.1.call-start = ((), (), s32[]{:S(2)}) async-start(), calls=%async_computation.13 | async-start | bytes 491520 | tf_op jit(solution)/shard_map/reduce_scatter | solution.py:118
  71.8 2.0 copy-start.14
  75.2 0.9 copy-start.7
  76.1 1.3 copy-start.4
  77.4 148.1 %all-gather.6.cloned.1.call-start = ((), (), s32[]{:S(2)}) async-start(), calls=%async_computation.14 | async-start | bytes 3932160 | tf_op jit(solution)/shard_map/all_gather | solution.py:158
  78.7 26.3 %copy-start.11 = (bf16[96,512]{1,0:T(8,128)(2,1)S(1)}, bf16[96,512]{1,0:T(8,128)(2,1)}, u32[]{:S(2)}) copy-start(bf16[96,512]{1,0:T(8,128)(2,1)} %param.24) | copy-start | bytes 294916
  117.2 97.3 %copy-start.2 = (bf16[384,512]{1,0:T(8,128)(2,1)}, bf16[384,512]{1,0:T(8,128)(2,1)S(1)}, u32[]{:S(2)}) copy-start(bf16[384,512]{1,0:T(8,128)(2,1)S(1)} %all_gather.24) | copy-start | bytes 1179652
  125.0 2.2 copy-start.1
  125.0 2.3 copy-start.3
  132.3 11.3 %copy-start.5 = (bf16[768,512]{1,0:T(8,128)(2,1)S(1)}, bf16[768,512]{1,0:T(8,128)(2,1)}, u32[]{:S(2)}) copy-start(bf16[768,512]{1,0:T(8,128)(2,1)} %param.25) | copy-start | bytes 2359300
  139.9 28.5 %all-to-all-start.7 = ((bf16[768,4,128]{0,2,1:T(8,128)(2,1)}), bf16[768,4,128]{0,2,1:T(8,128)(2,1)S(1)}, u32[]{:S(2)}, u32[]{:S(2)}) async-start(bf16[768,4,128]{0,2,1:T(8,128)(2,1)} %bitcast.35), calls=%async_computation.8 | async-start | bytes 1572864 | tf_op jit(solution)/shard_map/all_to_all | solution.py:76
  143.4 121.9 %all-gather.8.cloned.1.call-start = ((), (), s32[]{:S(2)}) async-start(), calls=%async_computation.15 | async-start | bytes 3932160 | tf_op jit(solution)/shard_map/all_gather | solution.py:159
  168.4 5.7 %copy-start.8 = (bf16[768,512]{0,1:T(8,128)(2,1)S(1)}, bf16[768,512]{0,1:T(8,128)(2,1)}, u32[]{:S(2)}) copy-start(bf16[768,512]{0,1:T(8,128)(2,1)} %copy-done.7) | copy-start | bytes 2359300
  168.4 23.2 %all-to-all-start.5 = ((bf16[768,4,128]{2,0,1:T(8,128)(2,1)}), bf16[768,4,128]{2,0,1:T(8,128)(2,1)}, u32[]{:S(2)}, u32[]{:S(2)}) async-start(bf16[768,4,128]{2,0,1:T(8,128)(2,1)} %copy_bitcast_fusion.1), calls=%async_computation.6 | async-start | bytes 1572864 | tf_op jit(solution)/shard_map/all_to_all | solution.py:78
  174.0 1.2 copy-start.15
  176.4 11.2 %copy-start.19 = (bf16[96,512]{1,0:T(8,128)(2,1)S(1)}, bf16[96,512]{1,0:T(8,128)(2,1)}, u32[]{:S(2)}) copy-start(bf16[96,512]{1,0:T(8,128)(2,1)} %reduce-scatter.2.cloned.1.call-done) | copy-start | bytes 294916
  191.6 19.6 %all-to-all-start.9 = ((bf16[96,4,128]{2,0,1:T(8,128)(2,1)}), bf16[96,4,128]{2,0,1:T(8,128)(2,1)S(1)}, u32[]{:S(2)}, u32[]{:S(2)}) async-start(bf16[96,4,128]{2,0,1:T(8,128)(2,1)} %copy_bitcast_fusion.4), calls=%async_computation.10 | async-start | bytes 196608 | tf_op jit(solution)/shard_map/all_to_all | solution.py:165
  211.2 9.1 %all-to-all-start.10 = ((bf16[96,4,128]{2,0,1:T(8,128)(2,1)}), bf16[96,4,128]{2,0,1:T(8,128)(2,1)S(1)}, u32[]{:S(2)}, u32[]{:S(2)}) async-start(bf16[96,4,128]{2,0,1:T(8,128)(2,1)} %copy_bitcast_fusion.3), calls=%async_computation.11 | async-start | bytes 196608 | tf_op jit(solution)/shard_map/all_to_all | solution.py:164
  220.3 40.1 %all-to-all-start.8 = ((bf16[768,4,128]{2,0,1:T(8,128)(2,1)}), bf16[768,4,128]{2,0,1:T(8,128)(2,1)}, u32[]{:S(2)}, u32[]{:S(2)}) async-start(bf16[768,4,128]{2,0,1:T(8,128)(2,1)} %copy.67), calls=%async_computation.9 | async-start | bytes 1572864 | tf_op jit(solution)/shard_map/all_to_all | solution.py:166
  225.5 4.0 %copy-start = (bf16[3072,512]{0,1:T(8,128)(2,1)S(1)}, bf16[3072,512]{0,1:T(8,128)(2,1)}, u32[]{:S(2)}) copy-start(bf16[3072,512]{0,1:T(8,128)(2,1)} %all-gather.6.cloned.1.call-done) | copy-start | bytes 9437188
  228.5 1.1 copy-start.9
  229.7 1.7 copy-start.10
  260.4 10.6 %all-to-all-start.3 = ((bf16[8,16,128]{2,1,0:T(8,128)(2,1)}), bf16[8,16,128]{2,1,0:T(8,128)(2,1)S(1)}, u32[]{:S(2)}, u32[]{:S(2)}) async-start(bf16[8,16,128]{2,1,0:T(8,128)(2,1)} %bitcast.26), calls=%async_computation.4 | async-start | bytes 65536 | tf_op jit(solution)/shard_map/all_to_all | solution.py:184
  265.2 65.7 %all-reduce.3.cloned.1.call-start = ((), (), s32[]{:S(2)}) async-start(), calls=%async_computation.16 | async-start | bytes 1835008 | tf_op jit(solution)/shard_map/psum | solution.py:205
  265.3 4.0 %copy-start.16 = (bf16[1,128,512]{1,2,0:T(8,128)(2,1)S(1)}, bf16[1,128,512]{1,2,0:T(8,128)(2,1)}, u32[]{:S(2)}) copy-start(bf16[1,128,512]{1,2,0:T(8,128)(2,1)} %fusion.15) | copy-start | bytes 393220
  265.3 4.0 %copy-start.17 = (bf16[1,128,512]{1,2,0:T(8,128)(2,1)S(1)}, bf16[1,128,512]{1,2,0:T(8,128)(2,1)}, u32[]{:S(2)}) copy-start(bf16[1,128,512]{1,2,0:T(8,128)(2,1)} %fusion.14) | copy-start | bytes 393220
  265.3 4.0 %copy-start.18 = (bf16[1,128,512]{1,2,0:T(8,128)(2,1)S(1)}, bf16[1,128,512]{1,2,0:T(8,128)(2,1)}, u32[]{:S(2)}) copy-start(bf16[1,128,512]{1,2,0:T(8,128)(2,1)} %fusion.13) | copy-start | bytes 393220
  269.4 1.6 copy-start.13
  273.0 9.1 %all-to-all-start.4 = ((bf16[4,96,128]{2,1,0:T(8,128)(2,1)}), bf16[4,96,128]{2,1,0:T(8,128)(2,1)S(1)}, u32[]{:S(2)}, u32[]{:S(2)}) async-start(bf16[4,96,128]{2,1,0:T(8,128)(2,1)} %bitcast.28), calls=%async_computation.5 | async-start | bytes 196608 | tf_op jit(solution)/shard_map/all_to_all | solution.py:197
  282.1 54.6 %all-to-all-start.6 = ((bf16[4,768,128]{2,1,0:T(8,128)(2,1)}), bf16[4,768,128]{2,1,0:T(8,128)(2,1)S(1)}, u32[]{:S(2)}, u32[]{:S(2)}) async-start(bf16[4,768,128]{2,1,0:T(8,128)(2,1)} %bitcast.176), calls=%async_computation.7 | async-start | bytes 1572864 | tf_op jit(solution)/shard_map/all_to_all | solution.py:200
  332.0 3.2 copy-start.21
  333.0 2.9 copy-start.20
Sparse Core Ops, SparseCore 0:
  10.4 55.0 all-gather.3
  77.5 23.4 reduce-scatter.1
  132.4 59.5 all-gather.5
  193.7 49.8 all-gather.7
  270.3 60.5 all-reduce.2
where the time goes:
time: 346 us; the launch traced here: 345 us
  waiting for transfers between devices  89.5 us (26%)
  local copies, waits for them, and re-layouts  59.3 us (17%)
  blocking collectives  54.9 us (16%)
  matrix products  45.6 us (13%)
  starting transfers between devices  41.6 us (12%)
  other arithmetic  39.4 us (11%)
  between operations  14.3 us (4%)
    psum x1, waiting for transfers between devices, shards(): lax.psum(jnp.stack([grad_edge_latent, grad_edge_sender, grad_edge_receive...  44.6 us
    reduce_scatter x1, waiting for transfers between devices, shards(): lax.psum_scatter(jnp.dot(row_incidence, edge_new_rows, preferred_element_...  22.3 us
    dot_general x7, matrix products, matmul_back(): lax.dot_general(first_operand, second_operand, (((1,), (1,)), ((), ())),...  18 us
    scatter-add x1, other arithmetic, shards(): jax.ops.segment_sum(sender_grad, sender_slot, num_segments=lookup_table.s...  17.3 us
    all_gather x1, blocking collectives, shards(): lookup_full = lax.all_gather(lookup_table, 'feat', axis=1, tiled=True)  15.3 us
    all_gather x1, blocking collectives, shards(): lax.all_gather(node_mix_grad_rows, 'feat', axis=0, tiled=True)  13.4 us
    dot_general x7, matrix products, transposed(): lax.dot_general(first_operand, second_operand, (((0,), (0,)), ((), ())),...  11.6 us
    gather x1, local copies, waits for them, and re-layouts, shards(): receivers = node_lat[receiver_row]  11.5 us
  transfers between devices with their start and end apart: 15, of which 8 were waited for; matrix products, arithmetic and copies ran while one was open for 31% of the time, Pallas kernels for 0%

commit v1 on v0

--- a/solution.py
+++ b/solution.py
@@ -202,11 +202,14 @@
         ).astype(edge_grad.dtype),
     )
     summed_grads = (
-        lax.psum(
-            jnp.stack([grad_edge_latent, grad_edge_sender, grad_edge_receiver], axis=0).astype(
-                jnp.bfloat16
+        jnp.sum(
+            lax.all_gather(
+                jnp.stack([grad_edge_latent, grad_edge_sender, grad_edge_receiver], axis=0).astype(
+                    jnp.bfloat16
+                ),
+                "region",
             ),
-            "region",
+            axis=0,
         ).astype(jnp.float32),
         lax.psum(grad_edge_second_layer.astype(jnp.bfloat16), "region").astype(jnp.float32),
         lax.psum(

time: 346 us -> 339 us (0.980)
  waiting for transfers between devices: 89.5 us -> 82.4 us
  blocking collectives: 54.9 us -> 48.4 us
    psum x1, waiting for transfers between devices: 44.6 us -> 0.01 us  [shards(): lax.psum(grad_edge_second_layer.astype(jnp.bfloat16), 'region')]
    all_to_all x1, waiting for transfers between devices: 0.01 us -> 16.5 us  [shards(): lax.all_to_all(edge_latent_rows, 'feat', split_axis=1, concat_axis=0, til...]
    all_gather x1, waiting for transfers between devices: 0.01 us -> 12.8 us  [shards(): lax.all_gather(pre_grad_rows, 'feat', axis=0, tiled=True)]
    all_to_all x1 -> x0, blocking collectives: 7.59 us -> none  [shards(): lax.all_to_all(node_cot_rows, 'feat', split_axis=1, concat_axis=0, tiled=...]
    all_to_all x1, waiting for transfers between devices: 0.01 us -> 5.7 us  [shards(): lax.all_to_all(edge_grad.astype(jnp.bfloat16), 'feat', split_axis=0, conc...]
    all_to_all x1, waiting for transfers between devices: 4.75 us -> 0.01 us  [shards(): lax.all_to_all(node_hidden_rows, 'feat', split_axis=1, concat_axis=0, til...]
    all_to_all x1, waiting for transfers between devices: 0.01 us -> 4.3 us  [shards(): lax.all_to_all(pooled_rows, 'feat', split_axis=1, concat_axis=0, tiled=True)]
    all_to_all x0 -> x1, waiting for transfers between devices: none -> 3.86 us  [shards(): lax.all_to_all(node_cot_rows, 'feat', split_axis=1, concat_axis=0, tiled=...]
  transfers between devices with their start and end apart: 15 -> 17, of which waited for: 8 -> 11; matrix products, arithmetic and copies ran while one was open for 31% -> 33% of each run, Pallas kernels for 0% -> 0%
where the time goes in v1:
time: 339 us; the launch traced here: 337 us
  waiting for transfers between devices  82.4 us (24%)
  local copies, waits for them, and re-layouts  62.2 us (18%)
  blocking collectives  48.4 us (14%)
  starting transfers between devices  44.4 us (13%)
  matrix products  42.9 us (13%)
  other arithmetic  42.6 us (13%)
  between operations  14.6 us (4%)
    reduce_scatter x1, waiting for transfers between devices, shards(): lax.psum_scatter(jnp.dot(row_incidence, edge_new_rows, preferred_element_...  22.3 us
    scatter-add x1, other arithmetic, shards(): jax.ops.segment_sum(sender_grad, sender_slot, num_segments=lookup_table.s...  17.3 us
    all_to_all x1, waiting for transfers between devices, shards(): lax.all_to_all(edge_latent_rows, 'feat', split_axis=1, concat_axis=0, til...  16.5 us
    dot_general x7, matrix products, matmul_back(): lax.dot_general(first_operand, second_operand, (((1,), (1,)), ((), ())),...  15.4 us
    all_gather x1, blocking collectives, shards(): lookup_full = lax.all_gather(lookup_table, 'feat', axis=1, tiled=True)  15.3 us
    all_gather x1, blocking collectives, shards(): lax.all_gather(node_mix_grad_rows, 'feat', axis=0, tiled=True)  14.4 us
    all_gather x1, waiting for transfers between devices, shards(): lax.all_gather(pre_grad_rows, 'feat', axis=0, tiled=True)  12.8 us
    gather x1, local copies, waits for them, and re-layouts, shards(): receivers = node_lat[receiver_row]  11.5 us
  transfers between devices with their start and end apart: 17, of which 11 were waited for; matrix products, arithmetic and copies ran while one was open for 33% of the time, Pallas kernels for 0%

profile of v1, /device:TPU:0, one launch (start us, length us, event | category | flops | bytes accessed | tf_op | source)
XLA Modules:
  0.0 337.5 jit_solution(17380627588632279719)
XLA Ops:
  7.2 2.3 pad_maximum_fusion
  10.3 5.2 %all-to-all-start = ((bf16[96,4,128]{2,0,1:T(8,128)(2,1)}), bf16[96,4,128]{2,0,1:T(8,128)(2,1)S(1)}, u32[]{:S(2)}, u32[]{:S(2)}) async-start(bf16[96,4,128]{2,0,1:T(8,128)(2,1)} %copy_bitcast_fusion.6), calls=%async_computation | async-start | bytes 196608 | tf_op jit(solution)/shard_map/all_to_all | solution.py:75
  16.7 8.7 %all_gather.27 = f32[2,512]{1,0:T(2,128)S(1)} all-gather(f32[2,128]{1,0:T(2,128)S(1)} %pad_maximum_fusion.4), channel_id=1, replica_groups=mesh['region'=8,'feat'=4] {'feat'}, dimensions={1}, use_global_device_ids=true | all-gather | bytes 5120 | tf_op jit(solution)/shard_map/all_gather | solution.py:98
  27.0 4.9 %all-to-all-start.1 = ((bf16[8,16,128]{2,1,0:T(8,128)(2,1)}), bf16[8,16,128]{2,1,0:T(8,128)(2,1)S(1)}, u32[]{:S(2)}, u32[]{:S(2)}) async-start(bf16[8,16,128]{2,1,0:T(8,128)(2,1)} %bitcast.10), calls=%async_computation.1 | async-start | bytes 65536 | tf_op jit(solution)/shard_map/all_to_all | solution.py:90
  32.0 5.7 %all-to-all-done.1 = bf16[8,16,128]{2,1,0:T(8,128)(2,1)S(1)} async-done(((bf16[8,16,128]{2,1,0:T(8,128)(2,1)}), bf16[8,16,128]{2,1,0:T(8,128)(2,1)S(1)}, u32[]{:S(2)}, u32[]{:S(2)}) %all-to-all-start.1) | async-done | bytes 32800 | tf_op jit(solution)/shard_map/all_to_all | solution.py:90
  37.7 15.3 %all_gather.26 = bf16[512,512]{1,0:T(8,128)(2,1)S(1)} all-gather(bf16[512,128]{1,0:T(8,128)(2,1)S(1)} %pad_maximum_fusion.3), channel_id=1, replica_groups=mesh['region'=8,'feat'=4] {'feat'}, dimensions={1}, use_global_device_ids=true | all-gather | bytes 655360 | tf_op jit(solution)/shard_map/all_gather | solution.py:101
  53.0 3.3 gather_fusion.2
  56.3 2.7 gather_fusion.1
  59.0 6.5 %all-gather.5.cloned.1.call-done = bf16[7,512,512]{2,1,0:T(8,128)(2,1)} async-done(((bf16[7,128,512]{2,1,0:T(8,128)(2,1)}), bf16[7,512,512]{2,1,0:T(8,128)(2,1)}) %all-gather.5.cloned.1.call-update) | async-done | bytes 3670032 | tf_op jit(solution)/shard_map/all_gather | solution.py:97
  67.1 1.7 fusion.17
  68.9 3.0 multiply_convert_fusion.2
  71.9 2.0 fusion.42
  78.8 22.3 %reduce-scatter.2.cloned.1.call-done = bf16[96,512]{1,0:T(8,128)(2,1)} async-done(((bf16[384,512]{1,0:T(8,128)(2,1)}), bf16[96,512]{1,0:T(8,128)(2,1)}) %reduce-scatter.2.cloned.1.call-update) | async-done | bytes 98320 | tf_op jit(solution)/shard_map/reduce_scatter | solution.py:118
  107.4 9.9 %all_gather.28 = bf16[384,512]{1,0:T(8,128)(2,1)S(1)} all-gather(bf16[96,512]{1,0:T(8,128)(2,1)S(1)} %fusion.10), channel_id=1, replica_groups=mesh['region'=8,'feat'=4] {'feat'}, dimensions={0}, use_global_device_ids=true | all-gather | bytes 491520 | tf_op jit(solution)/shard_map/all_gather | solution.py:146
  118.9 3.1 gather_fusion.3
  122.0 3.0 copy.75
  125.1 2.2 fusion.41
  128.9 3.5 %multiply_convert_fusion = bf16[768,512]{0,1:T(8,128)(2,1)} fusion(f32[768,512]{0,1:T(8,128)} %get-tuple-element.62, bf16[768,512]{0,1:T(8,128)(2,1)} %multiply_convert_fusion.1, bf16[7,512,512]{2,1,0:T(8,128)(2,1)} %all-gather.5.cloned.1.call-done), kind=kOutput, calls=%fused_computation.22 | convolution fusion | flops 406192128 | bytes 3670016 | tf_op jit(solution)/shard_map/dot_general | solution.py:38
  132.5 3.7 %all-to-all-start.7 = ((bf16[768,4,128]{0,2,1:T(8,128)(2,1)}), bf16[768,4,128]{0,2,1:T(8,128)(2,1)S(1)}, u32[]{:S(2)}, u32[]{:S(2)}) async-start(bf16[768,4,128]{0,2,1:T(8,128)(2,1)} %bitcast.35), calls=%async_computation.8 | async-start | bytes 1572864 | tf_op jit(solution)/shard_map/all_to_all | solution.py:76
  136.8 16.5 %all-to-all-done.7 = bf16[768,4,128]{0,2,1:T(8,128)(2,1)S(1)} async-done(((bf16[768,4,128]{0,2,1:T(8,128)(2,1)}), bf16[768,4,128]{0,2,1:T(8,128)(2,1)S(1)}, u32[]{:S(2)}, u32[]{:S(2)}) %all-to-all-start.7) | async-done | bytes 786464 | tf_op jit(solution)/shard_map/all_to_all | solution.py:76
  153.3 3.3 all-to-all-start.9
  157.3 4.3 %all-to-all-done.9 = bf16[96,4,128]{2,0,1:T(8,128)(2,1)S(1)} async-done(((bf16[96,4,128]{2,0,1:T(8,128)(2,1)}), bf16[96,4,128]{2,0,1:T(8,128)(2,1)S(1)}, u32[]{:S(2)}, u32[]{:S(2)}) %all-to-all-start.9) | async-done | bytes 98336 | tf_op jit(solution)/shard_map/all_to_all | solution.py:165
  161.6 3.5 %all-to-all-start.10 = ((bf16[96,4,128]{2,0,1:T(8,128)(2,1)}), bf16[96,4,128]{2,0,1:T(8,128)(2,1)S(1)}, u32[]{:S(2)}, u32[]{:S(2)}) async-start(bf16[96,4,128]{2,0,1:T(8,128)(2,1)} %copy_bitcast_fusion.3), calls=%async_computation.11 | async-start | bytes 196608 | tf_op jit(solution)/shard_map/all_to_all | solution.py:164
  165.1 11.5 %gather_fusion.6 = bf16[3072,128]{1,0:T(8,128)(2,1)} fusion(bf16[384,128]{1,0:T(8,128)(2,1)S(1)} %bitcast.174, s32[3072]{0:T(1024)S(1)} %fusion.38), kind=kCustom, calls=%fused_computation.6 | custom fusion | bytes 1585152 | tf_op jit(solution)/shard_map/gather | solution.py:93
  176.7 11.5 %gather_fusion.5 = bf16[3072,128]{1,0:T(8,128)(2,1)} fusion(bf16[512,128]{1,0:T(8,128)(2,1)S(1)} %pad_maximum_fusion.3, s32[3072]{0:T(1024)S(1)} %fusion.39), kind=kCustom, calls=%fused_computation.5 | custom fusion | bytes 1585152 | tf_op jit(solution)/shard_map/gather | solution.py:92
  188.6 2.4 copy.86
  191.0 3.9 %all-to-all-start.8 = ((bf16[768,4,128]{2,0,1:T(8,128)(2,1)}), bf16[768,4,128]{2,0,1:T(8,128)(2,1)S(1)}, u32[]{:S(2)}, u32[]{:S(2)}) async-start(bf16[768,4,128]{2,0,1:T(8,128)(2,1)} %copy.86), calls=%async_computation.9 | async-start | bytes 1572864 | tf_op jit(solution)/shard_map/all_to_all | solution.py:166
  195.2 14.4 %all_gather.32 = bf16[384,512]{1,0:T(8,128)(2,1)S(1)} all-gather(bf16[96,512]{1,0:T(8,128)(2,1)S(1)} %get-tuple-element.53), channel_id=1, replica_groups=mesh['region'=8,'feat'=4] {'feat'}, dimensions={0}, use_global_device_ids=true | all-gather | bytes 491520 | tf_op jit(solution)/shard_map/all_gather | solution.py:147
  211.6 3.7 %convolution_convert_fusion.6 = bf16[128,512]{1,0:T(8,128)(2,1)} fusion(bf16[3072,128]{1,0:T(8,128)(2,1)S(1)} %bitcast.179, bf16[3072,512]{0,1:T(8,128)(2,1)} %all-gather.11.cloned.1.call-done), kind=kOutput, calls=%fused_computation.45 | convolution fusion | flops 402718720 | bytes 4063232 | tf_op jit(solution)/shard_map/dot_general | solution.py:44
  215.4 12.8 %all-gather.7.cloned.1.call-done = bf16[3072,512]{0,1:T(8,128)(2,1)} async-done(((bf16[768,512]{0,1:T(8,128)(2,1)}), bf16[3072,512]{0,1:T(8,128)(2,1)}) %all-gather.7.cloned.1.call-update) | async-done | bytes 3145744 | tf_op jit(solution)/shard_map/all_gather | solution.py:158
  228.2 3.2 fusion.15
  235.1 3.3 all-to-all-start.2
  239.4 3.9 %all-to-all-done.2 = bf16[96,4,128]{2,0,1:T(8,128)(2,1)S(1)} async-done(((bf16[96,4,128]{2,0,1:T(8,128)(2,1)}), bf16[96,4,128]{2,0,1:T(8,128)(2,1)S(1)}, u32[]{:S(2)}, u32[]{:S(2)}) %all-to-all-start.2) | async-done | bytes 98336 | tf_op jit(solution)/shard_map/all_to_all | solution.py:77
  243.3 4.2 %all-to-all-start.5 = ((bf16[768,4,128]{2,0,1:T(8,128)(2,1)}), bf16[768,4,128]{2,0,1:T(8,128)(2,1)}, u32[]{:S(2)}, u32[]{:S(2)}) async-start(bf16[768,4,128]{2,0,1:T(8,128)(2,1)} %copy_bitcast_fusion.1), calls=%async_computation.6 | async-start | bytes 1572864 | tf_op jit(solution)/shard_map/all_to_all | solution.py:78
  249.5 10.9 %gather_fusion.4 = f32[3072,128]{1,0:T(8,128)} fusion(f32[384,128]{1,0:T(8,128)S(1)} %constant_dynamic-slice_fusion, s32[3072]{0:T(1024)S(1)} %fusion.38), kind=kCustom, calls=%fused_computation.4 | custom fusion | bytes 3158016 | tf_op jit(solution)/shard_map/gather | solution.py:162
  260.4 3.1 bitcast_add_fusion
  263.5 2.4 fusion.45
  265.9 2.2 fusion.25
  268.1 17.3 %scatter_custom_fusion = f32[512,128]{1,0:T(8,128)S(1)} fusion(s32[3072]{0:T(1024)S(1)} %copy-done.24, f32[3072,128]{1,0:T(8,128)} %fusion.25, f32[]{:T(128)} %constant.21.clone.1), kind=kCustom, calls=%fused_computation.95 | custom fusion | flops 393216 | bytes 262656 | tf_op jit(solution)/shard_map/scatter-add | solution.py:182
  286.0 4.6 %all-to-all-start.3 = ((bf16[8,16,128]{2,1,0:T(8,128)(2,1)}), bf16[8,16,128]{2,1,0:T(8,128)(2,1)S(1)}, u32[]{:S(2)}, u32[]{:S(2)}) async-start(bf16[8,16,128]{2,1,0:T(8,128)(2,1)} %bitcast.26), calls=%async_computation.4 | async-start | bytes 65536 | tf_op jit(solution)/shard_map/all_to_all | solution.py:184
  290.6 2.6 fusion
  296.3 2.8 scatter_custom_fusion.1
  300.7 4.1 %all-to-all-start.4 = ((bf16[4,96,128]{2,1,0:T(8,128)(2,1)}), bf16[4,96,128]{2,1,0:T(8,128)(2,1)S(1)}, u32[]{:S(2)}, u32[]{:S(2)}) async-start(bf16[4,96,128]{2,1,0:T(8,128)(2,1)} %bitcast.28), calls=%async_computation.5 | async-start | bytes 196608 | tf_op jit(solution)/shard_map/all_to_all | solution.py:197
  304.8 3.4 %fusion.2 = bf16[3072,128]{1,0:T(8,128)(2,1)} fusion(f32[3072,128]{1,0:T(8,128)} %bitcast_add_fusion, bf16[3072,512]{0,1:T(8,128)(2,1)S(1)} %copy-done.1, bf16[3,128,512]{2,1,0:T(8,128)(2,1)} %param.18), kind=kOutput, calls=%fused_computation.13 | convolution fusion | flops 403439616 | bytes 5636096 | tf_op jit(solution)/shard_map/dot_general | solution.py:38
  309.8 3.5 %all-to-all-start.6 = ((bf16[4,768,128]{2,1,0:T(8,128)(2,1)}), bf16[4,768,128]{2,1,0:T(8,128)(2,1)S(1)}, u32[]{:S(2)}, u32[]{:S(2)}) async-start(bf16[4,768,128]{2,1,0:T(8,128)(2,1)} %bitcast.176), calls=%async_computation.7 | async-start | bytes 1572864 | tf_op jit(solution)/shard_map/all_to_all | solution.py:200
  317.5 5.7 %all-to-all-done.6 = bf16[4,768,128]{2,1,0:T(8,128)(2,1)S(1)} async-done(((bf16[4,768,128]{2,1,0:T(8,128)(2,1)}), bf16[4,768,128]{2,1,0:T(8,128)(2,1)S(1)}, u32[]{:S(2)}, u32[]{:S(2)}) %all-to-all-start.6) | async-done | bytes 786464 | tf_op jit(solution)/shard_map/all_to_all | solution.py:200
  324.5 2.2 all-gather.9.cloned.1.call-done
  326.7 2.4 reduce_sum.92
  (140 shorter events, 44.0 us)
Async XLA Ops:
  7.2 2.4 copy-start.15
  7.2 58.3 %all-gather.5.cloned.1.call-start = ((), (), s32[]{:S(2)}) async-start(), calls=%async_computation.12 | async-start | bytes 4587520 | tf_op jit(solution)/shard_map/all_gather | solution.py:97
  7.2 8.2 %copy-start.8 = (bf16[768,512]{1,0:T(8,128)(2,1)S(1)}, bf16[768,512]{1,0:T(8,128)(2,1)}, u32[]{:S(2)}) copy-start(bf16[768,512]{1,0:T(8,128)(2,1)} %param.14) | copy-start | bytes 2359300
  9.6 7.1 %copy-start.25 = (s32[1,8,16]{2,1,0:T(8,128)S(1)}, s32[1,8,16]{2,1,0:T(8,128)}, u32[]{:S(2)}) copy-start(s32[1,8,16]{2,1,0:T(8,128)} %param.17) | copy-start | bytes 1540
  9.6 7.2 %copy-start.26 = (f32[128]{0:T(128)S(1)}, f32[128]{0:T(128)}, u32[]{:S(2)}) copy-start(f32[128]{0:T(128)} %param.23) | copy-start | bytes 1540
  9.6 7.2 %copy-start.27 = (f32[128]{0:T(128)S(1)}, f32[128]{0:T(128)}, u32[]{:S(2)}) copy-start(f32[128]{0:T(128)} %param.22) | copy-start | bytes 1540
  9.6 15.9 %copy-start.23 = (s32[3072]{0:T(1024)S(1)}, s32[3072]{0:T(1024)}, u32[]{:S(2)}) copy-start(s32[3072]{0:T(1024)} %param.15) | copy-start | bytes 36868
  9.6 16.0 %copy-start.24 = (s32[3072]{0:T(1024)S(1)}, s32[3072]{0:T(1024)}, u32[]{:S(2)}) copy-start(s32[3072]{0:T(1024)} %param.16) | copy-start | bytes 36868
  10.3 15.4 %all-to-all-start = ((bf16[96,4,128]{2,0,1:T(8,128)(2,1)}), bf16[96,4,128]{2,0,1:T(8,128)(2,1)S(1)}, u32[]{:S(2)}, u32[]{:S(2)}) async-start(bf16[96,4,128]{2,0,1:T(8,128)(2,1)} %copy_bitcast_fusion.6), calls=%async_computation | async-start | bytes 196608 | tf_op jit(solution)/shard_map/all_to_all | solution.py:75
  27.0 10.7 %all-to-all-start.1 = ((bf16[8,16,128]{2,1,0:T(8,128)(2,1)}), bf16[8,16,128]{2,1,0:T(8,128)(2,1)S(1)}, u32[]{:S(2)}, u32[]{:S(2)}) async-start(bf16[8,16,128]{2,1,0:T(8,128)(2,1)} %bitcast.10), calls=%async_computation.1 | async-start | bytes 65536 | tf_op jit(solution)/shard_map/all_to_all | solution.py:90
  31.9 69.2 %reduce-scatter.2.cloned.1.call-start = ((), (), s32[]{:S(2)}) async-start(), calls=%async_computation.13 | async-start | bytes 491520 | tf_op jit(solution)/shard_map/reduce_scatter | solution.py:118
  67.1 1.8 copy-start.16
  71.9 2.0 copy-start.18
  75.3 0.9 copy-start.9
  76.2 1.3 copy-start.6
  77.5 134.1 %all-gather.11.cloned.1.call-start = ((), (), s32[]{:S(2)}) async-start(), calls=%async_computation.16 | async-start | bytes 3932160 | tf_op jit(solution)/shard_map/all_gather | solution.py:159
  78.8 26.3 %copy-start.14 = (bf16[96,512]{1,0:T(8,128)(2,1)S(1)}, bf16[96,512]{1,0:T(8,128)(2,1)}, u32[]{:S(2)}) copy-start(bf16[96,512]{1,0:T(8,128)(2,1)} %param.24) | copy-start | bytes 294916
  117.3 92.3 %copy-start.3 = (bf16[384,512]{1,0:T(8,128)(2,1)}, bf16[384,512]{1,0:T(8,128)(2,1)S(1)}, u32[]{:S(2)}) copy-start(bf16[384,512]{1,0:T(8,128)(2,1)S(1)} %all_gather.28) | copy-start | bytes 1179652
  125.1 2.2 copy-start.2
  125.1 2.3 copy-start.5
  128.9 99.3 %all-gather.7.cloned.1.call-start = ((), (), s32[]{:S(2)}) async-start(), calls=%async_computation.14 | async-start | bytes 3932160 | tf_op jit(solution)/shard_map/all_gather | solution.py:158
  132.4 3.7 %copy-start.20 = (bf16[96,512]{1,0:T(8,128)(2,1)S(1)}, bf16[96,512]{1,0:T(8,128)(2,1)}, u32[]{:S(2)}) copy-start(bf16[96,512]{1,0:T(8,128)(2,1)} %reduce-scatter.2.cloned.1.call-done) | copy-start | bytes 294916
  132.5 20.8 %all-to-all-start.7 = ((bf16[768,4,128]{0,2,1:T(8,128)(2,1)}), bf16[768,4,128]{0,2,1:T(8,128)(2,1)S(1)}, u32[]{:S(2)}, u32[]{:S(2)}) async-start(bf16[768,4,128]{0,2,1:T(8,128)(2,1)} %bitcast.35), calls=%async_computation.8 | async-start | bytes 1572864 | tf_op jit(solution)/shard_map/all_to_all | solution.py:76
  153.3 8.3 %all-to-all-start.9 = ((bf16[96,4,128]{2,0,1:T(8,128)(2,1)}), bf16[96,4,128]{2,0,1:T(8,128)(2,1)S(1)}, u32[]{:S(2)}, u32[]{:S(2)}) async-start(bf16[96,4,128]{2,0,1:T(8,128)(2,1)} %copy_bitcast_fusion.4), calls=%async_computation.10 | async-start | bytes 196608 | tf_op jit(solution)/shard_map/all_to_all | solution.py:165
  161.6 29.3 %all-to-all-start.10 = ((bf16[96,4,128]{2,0,1:T(8,128)(2,1)}), bf16[96,4,128]{2,0,1:T(8,128)(2,1)S(1)}, u32[]{:S(2)}, u32[]{:S(2)}) async-start(bf16[96,4,128]{2,0,1:T(8,128)(2,1)} %copy_bitcast_fusion.3), calls=%async_computation.11 | async-start | bytes 196608 | tf_op jit(solution)/shard_map/all_to_all | solution.py:164
  191.0 20.6 %all-to-all-start.8 = ((bf16[768,4,128]{2,0,1:T(8,128)(2,1)}), bf16[768,4,128]{2,0,1:T(8,128)(2,1)S(1)}, u32[]{:S(2)}, u32[]{:S(2)}) async-start(bf16[768,4,128]{2,0,1:T(8,128)(2,1)} %copy.86), calls=%async_computation.9 | async-start | bytes 1572864 | tf_op jit(solution)/shard_map/all_to_all | solution.py:166
  194.9 119.1 %all-reduce.3.cloned.1.call-start = ((), (), s32[]{:S(2)}) async-start(), calls=%async_computation.17 | async-start | bytes 1048576 | tf_op jit(solution)/shard_map/psum | solution.py:214
  215.3 16.1 %copy-start.11 = (bf16[3072,128]{1,0:T(8,128)(2,1)S(1)}, bf16[3072,128]{1,0:T(8,128)(2,1)}, u32[]{:S(2)}) copy-start(bf16[3072,128]{1,0:T(8,128)(2,1)} %gather_fusion.5) | copy-start | bytes 2359300
  215.4 111.4 %all-gather.9.cloned.1.call-start = ((), (), s32[]{:S(2)}) async-start(), calls=%async_computation.15 | async-start | bytes 3538944 | tf_op jit(solution)/shard_map/all_gather | solution.py:206
  228.2 3.2 copy-start
  233.4 5.0 %copy-start.7 = (bf16[768,512]{1,0:T(8,128)(2,1)S(1)}, bf16[768,512]{1,0:T(8,128)(2,1)}, u32[]{:S(2)}) copy-start(bf16[768,512]{1,0:T(8,128)(2,1)} %param.25) | copy-start | bytes 2359300
  235.1 8.2 %all-to-all-start.2 = ((bf16[96,4,128]{2,0,1:T(8,128)(2,1)}), bf16[96,4,128]{2,0,1:T(8,128)(2,1)S(1)}, u32[]{:S(2)}, u32[]{:S(2)}) async-start(bf16[96,4,128]{2,0,1:T(8,128)(2,1)} %copy_bitcast_fusion.5), calls=%async_computation.3 | async-start | bytes 196608 | tf_op jit(solution)/shard_map/all_to_all | solution.py:77
  238.4 9.9 %copy-start.10 = (bf16[768,512]{0,1:T(8,128)(2,1)S(1)}, bf16[768,512]{0,1:T(8,128)(2,1)}, u32[]{:S(2)}) copy-start(bf16[768,512]{0,1:T(8,128)(2,1)} %copy-done.9) | copy-start | bytes 2359300
  243.3 17.1 %all-to-all-start.5 = ((bf16[768,4,128]{2,0,1:T(8,128)(2,1)}), bf16[768,4,128]{2,0,1:T(8,128)(2,1)}, u32[]{:S(2)}, u32[]{:S(2)}) async-start(bf16[768,4,128]{2,0,1:T(8,128)(2,1)} %copy_bitcast_fusion.1), calls=%async_computation.6 | async-start | bytes 1572864 | tf_op jit(solution)/shard_map/all_to_all | solution.py:78
  260.4 3.1 copy-start.1
  260.4 3.1 copy-start.13
  286.0 10.3 %all-to-all-start.3 = ((bf16[8,16,128]{2,1,0:T(8,128)(2,1)}), bf16[8,16,128]{2,1,0:T(8,128)(2,1)S(1)}, u32[]{:S(2)}, u32[]{:S(2)}) async-start(bf16[8,16,128]{2,1,0:T(8,128)(2,1)} %bitcast.26), calls=%async_computation.4 | async-start | bytes 65536 | tf_op jit(solution)/shard_map/all_to_all | solution.py:184
  290.6 2.6 copy-start.12
  293.2 1.0 copy-start.4
  293.2 1.0 copy-start.17
  293.2 1.1 copy-start.19
  300.7 9.1 %all-to-all-start.4 = ((bf16[4,96,128]{2,1,0:T(8,128)(2,1)}), bf16[4,96,128]{2,1,0:T(8,128)(2,1)S(1)}, u32[]{:S(2)}, u32[]{:S(2)}) async-start(bf16[4,96,128]{2,1,0:T(8,128)(2,1)} %bitcast.28), calls=%async_computation.5 | async-start | bytes 196608 | tf_op jit(solution)/shard_map/all_to_all | solution.py:197
  309.8 13.4 %all-to-all-start.6 = ((bf16[4,768,128]{2,1,0:T(8,128)(2,1)}), bf16[4,768,128]{2,1,0:T(8,128)(2,1)S(1)}, u32[]{:S(2)}, u32[]{:S(2)}) async-start(bf16[4,768,128]{2,1,0:T(8,128)(2,1)} %bitcast.176), calls=%async_computation.7 | async-start | bytes 1572864 | tf_op jit(solution)/shard_map/all_to_all | solution.py:200
  314.0 2.0 copy-start.22
  314.0 2.8 copy-start.21
Sparse Core Ops, SparseCore 0:
  10.4 55.0 all-gather.4
  77.6 23.4 reduce-scatter.1
  129.0 50.0 all-gather.10
  180.8 47.3 all-gather.6
  231.1 56.7 all-reduce.2
  289.5 37.2 all-gather.8
